TPU v7x, 32 devices: a whole 2x2x4 slice. The times are simulated.
32 devices in a mesh: groups: 2 (over x), sph: 16 (over z, y, core).
Axes of the slice: x: 2, y: 2, z: 4, core: 2. Of those that a mesh axis runs over, the one named last changes fastest.
Arguments:
- positions: float32 [512, 3], P('sph'), may hold values from -8 to 8
- wave_vectors: float32 [256, 3], replicated, may hold values from -5 to 5
- pattern: float32 [2, 448, 256], replicated, may hold values from -6 to 6
- dir_index: int32 [64], P('groups'), parts along dimension 0, may hold values from 0 to 255
- mie: float32 [2, 448, 512], P(None, None, 'sph'), may hold values from -0.9 to 0.9
- trans_table: bfloat16 [8, 2, 448, 448], replicated, may hold values from -0.1875 to 0.1875
- pair_route: int32 [1024, 1], P('sph'), may hold values from 0 to 15; in each aligned block of 64 rows (0 to 63, 64 to 127, ...) at most 8 rows name the same one
- pair_source: int32 [1024], P('sph'), may hold values from 0 to 15
- pair_target: int32 [1024], P('sph'), may hold values from 0 to 15
- pair_class: int32 [1024], P('sph'), may hold values from 0 to 7
Outputs:
- scattered: bfloat16 [896, 32768], P(None, ('groups', 'sph')), parts along dimension 1
- extinction: float32 [64], P('groups'), parts along dimension 0
There are 2 independent parts, one for each index of `groups`. A program takes and returns all parts, laid end to end along the dimension named above; an argument that names none is the same for every part. Nothing has to cross between parts.
Inputs may be any that keep to these rules, and one draw needn't show every extreme that they name: `pair_route`: among the rows of one device no device is named by more than 8 pairs, and in every draw some device is named by exactly 8 of them.
All inputs are finite; a program needn't handle non-finite values.
Results may differ from a plain program's by a relative error of at most 0.0051.
Values may be sent and summed in bfloat16 or wider, within the bound.
A program may use at most 192 MiB of HBM per device.

v0:
```python
import functools

import jax
import jax.numpy as jnp
from jax import lax
from jax.experimental import pallas as pl
from jax.experimental.pallas import tpu as pltpu
from jax.sharding import PartitionSpec as P

BLOCK = 2
LANES = 128
HIGHEST = lax.Precision.HIGHEST


def round_up(value, unit):
    return -(-value // unit) * unit


MESH = pl.DeviceIdType.MESH


def gather_kernel(devices, mie, small, all_mie, all_small, send, recv, local):
    me = lax.axis_index("sph")
    chips = devices // 2
    chip, core = me // 2, me % 2
    other = chip * 2 + (1 - core)
    peers = [other] + [((chip + r) % chips) * 2 + core for r in range(1, chips)]
    barrier = pltpu.get_barrier_semaphore()
    for peer in peers:
        pl.semaphore_signal(barrier, inc=1, device_id={"sph": peer}, device_id_type=MESH)
    pl.semaphore_wait(barrier, chips)
    arrays = ((mie, all_mie), (small, all_small))

    def start(source, target, at, slot, peer):
        copy = pltpu.make_async_remote_copy(
            src_ref=source, dst_ref=target, send_sem=send.at[at, slot], recv_sem=recv.at[at, slot],
            device_id={"sph": peer}, device_id_type=MESH,
        )
        copy.start()
        return copy

    own = [pltpu.make_async_copy(a, out.at[me], local.at[i]) for i, (a, out) in enumerate(arrays)]
    first = {}
    for r in list(range(1, chips)) + [0]:
        for i, (a, out) in enumerate(arrays):
            first[i, r] = start(a, out.at[me], i, r, peers[r])
    for copy in own:
        copy.start()
    second = []
    for r in range(1, chips):
        origin = ((chip + chips - r) % chips) * 2 + core
        for i, (a, out) in enumerate(arrays):
            first[i, r].wait_recv()
            second.append(start(out.at[origin], out.at[origin], i, chips + r, other))
    for i in range(len(arrays)):
        first[i, 0].wait_recv()
    for copy in second:
        copy.wait_recv()
    for copy in own:
        copy.wait()
    for copy in list(first.values()) + second:
        copy.wait_send()


def gather_all(devices, mie_rows, small):
    spec = pl.BlockSpec(memory_space=pltpu.VMEM)
    anywhere = pl.BlockSpec(memory_space=pl.ANY)
    copies = pltpu.SemaphoreType.DMA((2, devices))
    return pl.pallas_call(
        functools.partial(gather_kernel, devices),
        out_shape=[jax.ShapeDtypeStruct((devices,) + a.shape, a.dtype) for a in (mie_rows, small)],
        in_specs=[spec, spec],
        out_specs=[anywhere, anywhere],
        scratch_shapes=[copies, copies, pltpu.SemaphoreType.DMA((2,))],
        compiler_params=pltpu.CompilerParams(collective_id=0, has_side_effects=True),
        name="gather",
    )(mie_rows, small)


def sum_kernel(devices, dirs, part, total, inbox, send, recv):
    me = lax.axis_index("sph")
    peers = [(me + r) % devices for r in range(1, devices)]
    barrier = pltpu.get_barrier_semaphore()
    for peer in peers:
        pl.semaphore_signal(barrier, inc=1, device_id={"sph": peer}, device_id_type=MESH)
    pl.semaphore_wait(barrier, devices - 1)
    copies = []
    for r, peer in enumerate(peers):
        copy = pltpu.make_async_remote_copy(
            src_ref=part, dst_ref=inbox.at[me], send_sem=send.at[r], recv_sem=recv.at[r],
            device_id={"sph": peer}, device_id_type=MESH,
        )
        copy.start()
        copies.append(copy)
    inbox[me] = part[...]
    for copy in copies:
        copy.wait_recv()
    row = jnp.sum(jnp.sum(inbox[...], 0), 0, keepdims=True)
    shift = LANES // 2
    while shift >= dirs:
        row = row + pltpu.roll(row, shift, 1)
        shift //= 2
    total[...] = row
    for copy in copies:
        copy.wait_send()


def sum_all(devices, dirs, part):
    spec = pl.BlockSpec(memory_space=pltpu.VMEM)
    copies = pltpu.SemaphoreType.DMA((devices,))
    return pl.pallas_call(
        functools.partial(sum_kernel, devices, dirs),
        out_shape=jax.ShapeDtypeStruct((1, LANES), jnp.float32),
        in_specs=[spec],
        out_specs=spec,
        scratch_shapes=[pltpu.VMEM((devices,) + part.shape, jnp.float32), copies, copies],
        compiler_params=pltpu.CompilerParams(collective_id=1, has_side_effects=True),
        name="extinction",
    )(part)


def field_kernel(
    dims, lists, table_hbm, mie_sent, phase_rows, pat_rows, pat_tile, mie, cosine, sine,
    scattered, ext, head, chain, phase_at, mie_at, matrix, mixed, acc, table, mie_rows, loaded,
):
    modes, wide, dirs, blocks, classes, step_blocks = dims
    step = pl.program_id(0)
    columns = BLOCK * dirs
    capacity = lists.shape[2]

    load = pltpu.make_async_copy(table_hbm, table, loaded)

    @pl.when(step == 0)
    def _():
        load.start()

        def clear(cell, carry):
            head[cell] = -1
            return carry

        lax.fori_loop(0, blocks * classes, clear, 0)

        def link(device, carry):
            for k in range(capacity):
                cell = lists[device, 0, k]
                slot = device * capacity + k

                @pl.when(cell >= 0)
                def _():
                    chain[slot] = head[cell]
                    head[cell] = slot
                    phase_at[slot] = lists[device, 1, k]
                    mie_at[slot] = lists[device, 2, k]

            return carry

        lax.fori_loop(0, lists.shape[0], link, 0)
        mie_rows[...] = mie_sent[...].astype(jnp.float32)

    def product(slot):
        start = mie_at[slot]
        spread = jnp.broadcast_to(
            phase_rows[pl.ds(phase_at[slot], 1), :], (2 * columns, 2 * columns)
        ).T
        reals, imags = [], []
        for j in range(BLOCK):
            row = mie_rows[pl.ds(start + j, 1), :]
            mr, mi = row[:, :wide], row[:, wide:]
            c = jnp.concatenate([spread[j * dirs : (j + 1) * dirs]] * (wide // LANES), 1)
            s = jnp.concatenate([spread[columns + j * dirs : columns + (j + 1) * dirs]] * (wide // LANES), 1)
            reals.append(c * mr - s * mi)
            imags.append(c * mi + s * mr)
        return jnp.concatenate(reals, 0), jnp.concatenate(imags, 0)

    def build(index, carry):
        kind, local = index // step_blocks, index % step_blocks
        first = head[kind * blocks + step * step_blocks + local]
        rows = pl.ds(pl.multiple_of(local * columns, columns), columns)
        left = pl.ds(pl.multiple_of(kind * 2 * wide, 2 * wide), wide)
        right = pl.ds(pl.multiple_of(kind * 2 * wide + wide, wide), wide)

        @pl.when(first < 0)
        def _():
            zero = jnp.zeros((columns, wide), mixed.dtype)
            mixed[rows, left] = zero
            mixed[rows, right] = zero

        def finish(yr, yi):
            pr, pi = pat_rows[0], pat_rows[1]
            mixed[rows, left] = (yr * pr - yi * pi).astype(mixed.dtype)
            mixed[rows, right] = (yr * pi + yi * pr).astype(mixed.dtype)

        second = chain[jnp.maximum(first, 0)]

        @pl.when((first >= 0) & (second < 0))
        def _():
            finish(*product(first))

        @pl.when((first >= 0) & (second >= 0))
        def _():
            yr, yi = product(first)
            acc[0] = yr
            acc[1] = yi

            def more(slot):
                yr, yi = product(slot)
                acc[0] += yr
                acc[1] += yi
                return chain[slot]

            lax.while_loop(lambda slot: slot >= 0, more, second)
            finish(acc[0], acc[1])

        return carry

    lax.fori_loop(0, classes * step_blocks, build, 0)

    @pl.when(step == 0)
    def _():
        load.wait()
        for kind in range(classes):
            at = kind * 2 * wide
            if wide > modes:
                for part in range(2):
                    end = at + (part + 1) * wide
                    matrix[:, end - LANES : end] = jnp.zeros((2 * modes, LANES), matrix.dtype)
            real, imag = table[kind, 0], table[kind, 1]
            matrix[:modes, at : at + modes] = real
            matrix[:modes, at + wide : at + wide + modes] = -imag
            matrix[modes:, at : at + modes] = imag
            matrix[modes:, at + wide : at + wide + modes] = real

    interaction = lax.dot_general(
        matrix[...], mixed[...], (((1,), (1,)), ((), ())), preferred_element_type=jnp.float32
    )
    width = step_blocks * columns
    per_step = width // dirs
    spheres = mie.shape[1]
    picked = (
        lax.broadcasted_iota(jnp.int32, (spheres, width), 0)
        == step * per_step + lax.broadcasted_iota(jnp.int32, (spheres, width), 1) // dirs
    ).astype(jnp.bfloat16)
    rest, spread_mie = mie[...], 0.0
    for _ in range(3):
        piece = rest.astype(jnp.bfloat16)
        rest = rest - piece.astype(jnp.float32)
        spread_mie += jnp.dot(piece, picked, preferred_element_type=jnp.float32)
    mr, mi = spread_mie[:modes], spread_mie[modes:]
    c, s = cosine[...], sine[...]
    pr = jnp.concatenate([pat_tile[0]] * (width // LANES), 1)
    pi = jnp.concatenate([pat_tile[1]] * (width // LANES), 1)
    inc_r = c * pr - s * pi
    inc_i = c * pi + s * pr
    total_r = inc_r + interaction[:modes]
    total_i = inc_i + interaction[modes:]
    out_r = mr * total_r - mi * total_i
    out_i = mr * total_i + mi * total_r
    scattered[:modes, :] = out_r.astype(scattered.dtype)
    scattered[modes:, :] = out_i.astype(scattered.dtype)
    terms = jnp.sum((inc_r * out_r + inc_i * out_i).reshape(modes // 8, 8, width), 0)
    part = sum(terms[:, at : at + LANES] for at in range(0, width, LANES))

    @pl.when(step == 0)
    def _():
        ext[...] = part

    @pl.when(step > 0)
    def _():
        ext[...] += part


def shards(
    positions, wave_vectors, pattern, dir_index, mie, trans_table, pair_route, pair_source,
    pair_target, pair_class,
):
    modes = pattern.shape[1]
    wide = round_up(modes, LANES)
    spheres = positions.shape[0]
    dirs = dir_index.shape[0]
    columns = BLOCK * dirs
    blocks = spheres // BLOCK
    classes = trans_table.shape[0]
    devices = lax.axis_size("sph")
    me = lax.axis_index("sph")
    pair_count = pair_source.shape[0]
    capacity = max(2, 2 * pair_count // devices)
    slots = devices * capacity
    tables = wave_vectors.shape[0]

    select = (jnp.arange(tables, dtype=jnp.int32)[:, None] == dir_index[None, :]).astype(jnp.float32)
    k = jnp.dot(select.T, wave_vectors, precision=HIGHEST)
    phases = (
        positions[:, 0:1] * k[None, :, 0]
        + positions[:, 1:2] * k[None, :, 1]
        + positions[:, 2:3] * k[None, :, 2]
    )
    cosine, sine = jnp.cos(phases), jnp.sin(phases)
    phase_rows = jnp.concatenate(
        [cosine.reshape(blocks, columns), sine.reshape(blocks, columns)], 1
    )
    dest = pair_route[:, 0]
    order = jnp.arange(pair_count, dtype=jnp.int32)
    rank = jnp.sum(
        ((dest[:, None] == dest[None, :]) & (order[None, :] < order[:, None])).astype(jnp.int32), 1
    )
    slot_of = dest * capacity + rank
    match = slot_of[:, None] == jnp.arange(slots, dtype=jnp.int32)[None, :]
    cell_of = pair_class * blocks + pair_target
    small_rows = round_up(blocks + 3, 8)
    entries = jnp.stack(
        [cell_of + 1, me * small_rows + pair_source, me * spheres + pair_source * BLOCK]
    )
    lists = jnp.sum(jnp.where(match[None], entries[:, :, None], 0), 1)
    lists = (lists - jnp.array([[1], [0], [0]], jnp.int32)).astype(jnp.float32)
    lists = jnp.pad(lists, ((0, small_rows - blocks - 3), (0, LANES - slots)))
    small = jnp.concatenate([phase_rows, lists], 0)
    mie_rows = jnp.pad(jnp.transpose(mie, (2, 0, 1)), ((0, 0), (0, 0), (0, wide - modes)))
    mie_rows = mie_rows.reshape(spheres, 2 * wide).astype(jnp.bfloat16)

    all_mie, all_small = gather_all(devices, mie_rows, small)
    mine = lax.dynamic_slice_in_dim(all_small[:, blocks : blocks + 3], me * capacity, capacity, 2)
    mine = mine.astype(jnp.int32)
    all_mie = all_mie.reshape(devices * spheres, 2 * wide)
    all_small = all_small.reshape(devices * small_rows, LANES)

    select_tile = jnp.concatenate([select] * (LANES // dirs), 1)
    pat_tile = jnp.einsum("cmt,td->cmd", pattern, select_tile, precision=HIGHEST)
    pat_rows = jnp.einsum("td,cmt->cdm", select, pattern, precision=HIGHEST)
    pat_rows = jnp.pad(jnp.concatenate([pat_rows] * BLOCK, 1), ((0, 0), (0, 0), (0, wide - modes)))

    step_blocks = 2 * LANES // columns
    width = step_blocks * columns
    once = pl.Buffered(1)

    def whole(array):
        zeros = (0,) * array.ndim
        return pl.BlockSpec(array.shape, lambda i, *_: zeros, pipeline_mode=once)

    flat_mie = mie.reshape(2 * modes, spheres)
    operands = (trans_table, all_mie, all_small, pat_rows, pat_tile, flat_mie)
    line = pl.BlockSpec((1, width), lambda i, *_: (0, i))
    depth = classes * 2 * wide
    scattered, ext = pl.pallas_call(
        functools.partial(field_kernel, (modes, wide, dirs, blocks, classes, step_blocks)),
        grid_spec=pltpu.PrefetchScalarGridSpec(
            num_scalar_prefetch=1,
            grid=(blocks // step_blocks,),
            in_specs=[pl.BlockSpec(memory_space=pl.ANY)] + [whole(x) for x in operands[1:]] + [line, line],
            out_specs=[
                pl.BlockSpec((2 * modes, width), lambda i, *_: (0, i)),
                pl.BlockSpec((8, LANES), lambda i, *_: (0, 0)),
            ],
            scratch_shapes=[
                pltpu.SMEM((blocks * classes,), jnp.int32),
                pltpu.SMEM((slots,), jnp.int32),
                pltpu.SMEM((slots,), jnp.int32),
                pltpu.SMEM((slots,), jnp.int32),
                pltpu.VMEM((2 * modes, depth), jnp.bfloat16),
                pltpu.VMEM((width, depth), jnp.bfloat16),
                pltpu.VMEM((2, columns, wide), jnp.float32),
                pltpu.VMEM(trans_table.shape, jnp.bfloat16),
                pltpu.VMEM(all_mie.shape, jnp.float32),
                pltpu.SemaphoreType.DMA(()),
            ],
        ),
        out_shape=[
            jax.ShapeDtypeStruct((2 * modes, spheres * dirs), jnp.bfloat16),
            jax.ShapeDtypeStruct((8, LANES), jnp.float32),
        ],
        compiler_params=pltpu.CompilerParams(
            dimension_semantics=("arbitrary",), vmem_limit_bytes=60 * 1024 * 1024
        ),
        name="field",
    )(mine, *operands, cosine.reshape(1, spheres * dirs), sine.reshape(1, spheres * dirs))
    return (scattered, sum_all(devices, dirs, ext)[0, :dirs])


def solution(mesh):
    placed = (
        P("sph", None), P(), P(), P("groups"), P(None, None, "sph"), P(),
        P("sph", None), P("sph"), P("sph"), P("sph"),
    )
    return jax.shard_map(
        shards,
        mesh=mesh,
        in_specs=placed,
        out_specs=(P(None, ("groups", "sph")), P("groups")),
        check_vma=False,
    )
```

profile of v0, /device:TPU:0, one launch (start us, length us, event | category | flops | bytes accessed | tf_op | source)
XLA Modules:
  0.0 93.9 jit_solution(1399954337344931819)
XLA Ops:
  0.6 0.0 copy-start
  0.6 0.9 convert_reduce_fusion
  1.6 0.7 fusion.12
  2.2 0.7 add_bitcast_fusion.3
  3.0 0.9 fusion.6
  3.8 0.1 mul.168
  3.9 0.1 mul.184
  4.0 0.1 mul.176
  4.1 0.8 slice_bitcast_fusion.6
  4.9 0.1 iota_compare_fusion.3
  5.0 0.1 select_reduce_fusion
  5.1 0.7 add_convert_fusion
  5.8 0.1 mul.171
  5.9 0.1 mul.172
  6.0 0.1 mul.173
  6.1 0.1 mul.179
  6.1 0.1 mul.180
  6.2 0.1 mul.181
  6.3 0.1 mul.163
  6.4 0.1 mul.164
  6.5 0.1 mul.165
  6.6 0.1 fusion.14
  6.7 0.7 select_maximum_fusion.1.small
  7.4 0.1 fusion.10
  7.5 0.7 sin.18.sine
  8.2 0.7 cos.18.cosine
  8.9 0.7 iota_compare_fusion.1
  9.6 0.9 convert_bitcast_fusion
  10.5 0.1 copy.24
  10.5 0.1 pad.13.clone
  10.6 0.6 copy.25
  11.3 0.0 copy-done
  11.3 1.2 %convolution_bitcast_fusion.1 = f32[2,32,448]{2,1,0:T(8,128)S(1)} fusion(f32[2,448,256]{2,1,0:T(8,128)S(1)} %copy-done, s32[32]{0:T(128)} %param.14), kind=kOutput, calls=%fused_computation.1 | convolution fusion | flops 88096768 | bytes 1032320 | tf_op jit(solution)/shard_map/td,cmt->cdm/dot_general | solution.py:328
  12.5 0.7 select_maximum_fusion.pat_rows
  13.2 1.5 %convolution_bitcast_fusion.pat_tile = f32[2,448,128]{2,1,0:T(8,128)} fusion(f32[2,448,256]{2,1,0:T(8,128)S(1)} %copy-done, pred[256,32]{1,0:T(32,128)(4,1)S(1)} %iota_compare_fusion.1), kind=kOutput, calls=%fused_computation | convolution fusion | flops 352419840 | bytes 1384448 | tf_op jit(solution)/shard_map/cmt,td->cmd/dot_general | solution.py:327
  14.7 1.9 %copy.21 = f32[2,448,32]{2,1,0:T(8,128)} copy(f32[2,448,32]{1,2,0:T(8,128)} %param.15) | data formatting | bytes 229376 | tf_op args[4]
  16.5 19.0 %gather.1 = (bf16[16,32,1024]{2,1,0:T(8,128)(2,1)}, f32[16,24,128]{2,1,0:T(8,128)}) custom-call(bf16[32,1024]{1,0:T(8,128)(2,1)} %bitcast.50, f32[24,128]{1,0:T(8,128)} %select_maximum_fusion.1.small), custom_call_target="tpu_custom_call" | custom-call | tf_op jit(solution)/shard_map/gather/pallas_call | solution.py:69
  35.6 0.8 slice.30
  36.4 0.7 dynamic-slice_convert_fusion.lists
  37.1 34.6 %field.1 = (bf16[896,1024]{1,0:T(8,128)(2,1)}, f32[8,128]{1,0:T(8,128)}) custom-call(s32[16,3,8]{2,1,0:T(4,128)} %dynamic-slice_convert_fusion.lists, bf16[8,2,448,448]{3,2,1,0:T(8,128)(2,1)} %table_hbm.1, bf16[512,1024]{1,0:T(8,128)(2,1)} %bitcast.48, f32[384,128]{1,0:T(8,128)} %bitcast.49, f32[2,64,512]{2,1,0:T(8,128)} %select_maximum_fusion.pat_rows, ...), custom_call_target="tpu_custom_call" | custom-call | tf_op jit(solution)/shard_map/field/pallas_call | solution.py:343
  71.7 21.0 %extinction.1 = f32[1,128]{1,0:T(1,128)} custom-call(f32[8,128]{1,0:T(8,128)} %get-tuple-element.9.part), custom_call_target="tpu_custom_call" | custom-call | tf_op jit(solution)/shard_map/extinction/pallas_call | solution.py:111
  92.7 1.2 %slice_bitcast_fusion = f32[32]{0:T(128)} fusion(f32[1,128]{1,0:T(1,128)} %extinction.1), kind=kLoop, calls=%fused_computation.33 | loop fusion | bytes 256 | tf_op jit(solution)/shard_map/squeeze | solution.py:375
  (6 shorter events, 0.1 us)
Async XLA Ops:
  0.6 10.6 %copy-start = (f32[2,448,256]{2,1,0:T(8,128)S(1)}, f32[2,448,256]{2,1,0:T(8,128)}, u32[]{:S(2)}) copy-start(f32[2,448,256]{2,1,0:T(8,128)} %param.13) | copy-start | bytes 2752516
where the time goes:
time: 95 us; the launch traced here: 93.9 us
  Pallas kernels  74.6 us (79%)
  local copies, waits for them, and re-layouts  7.9 us (8%)
  other arithmetic  7.1 us (7%)
  matrix products  3.56 us (4%)
    pallas_call x1, Pallas kernels, shards(): pl.pallas_call(functools.partial(field_kernel, (modes, wide, dirs, blocks...  34.6 us
    pallas_call x1, Pallas kernels, sum_all(): pl.pallas_call(functools.partial(sum_kernel, devices, dirs), out_shape=ja...  21 us
    pallas_call x1, Pallas kernels, gather_all(): pl.pallas_call(functools.partial(gather_kernel, devices), out_shape=[jax....  19 us
    unnamed x5, local copies, waits for them, and re-layouts  2.58 us

commit v1 on v0

v1 whole, which is shorter than its diff:
```python
import functools

import jax
import jax.numpy as jnp
from jax import lax
from jax.experimental import pallas as pl
from jax.experimental.pallas import tpu as pltpu
from jax.sharding import PartitionSpec as P

BLOCK = 2
LANES = 128
HIGHEST = lax.Precision.HIGHEST
MESH = pl.DeviceIdType.MESH
F32 = jnp.float32
BF16 = jnp.bfloat16
ORDER = ((0, 2, 1, 3), (3, 0, 2, 1))


def sincos(angle):
    turns = jnp.floor(angle * 0.6366197723675814 + 0.5)
    rest = angle - turns * 1.5703125
    rest = rest - turns * 4.837512969970703125e-4
    rest = rest - turns * 7.54978995489188216e-8
    square = rest * rest
    sine = rest + rest * square * (
        -1.6666654611e-1 + square * (8.3321608736e-3 + square * -1.9515295891e-4)
    )
    cosine = 1.0 - 0.5 * square + square * square * (
        4.166664568298827e-2 + square * (-1.388731625493765e-3 + square * 2.443315711809948e-5)
    )
    quarter = turns.astype(jnp.int32)
    swap = (quarter & 1) == 1
    c = jnp.where(swap, sine, cosine)
    s = jnp.where(swap, cosine, sine)
    c = jnp.where(((quarter + 1) & 2) == 2, -c, c)
    s = jnp.where((quarter & 2) == 2, -s, s)
    return c, s


def split_two(x):
    high = x.astype(BF16)
    return high, (x - high.astype(F32)).astype(BF16)


def fused_kernel(
    dims, route, source, target, kind, pos_s, pos_v, wave_s, dir_s, mie, pattern_hbm, table_hbm,
    scattered, ext,
    table, pattern, t_real, t_diff, t_sum, all_mie, all_small, weights, x_real, x_imag, x_sum,
    pat, inc, spread, own_e, phase, delta, y_at, out_at, part, inbox,
    loaded, stored, send, recv, ext_send, ext_recv,
):
    modes, dirs, spheres, blocks, classes, devices, capacity = dims
    me = lax.axis_index("sph")
    chips = devices // 2
    chip, core = me // 2, me % 2
    other = chip * 2 + (1 - core)
    bits = []
    bit = chips // 2
    while bit >= 1:
        bits.append(bit)
        bit //= 2

    def flip(value, bit):
        return value + bit - 2 * bit * ((value // bit) % 2)

    partners = [flip(chip, bit) * 2 + core for bit in bits] + [other]
    everyone = [(me + r) % devices for r in range(1, devices)]

    barrier = pltpu.get_barrier_semaphore()
    for peer in partners:
        pl.semaphore_signal(barrier, inc=1, device_id={"sph": peer}, device_id_type=MESH)
    load_table = pltpu.make_async_copy(table_hbm, table, loaded.at[0])
    load_pattern = pltpu.make_async_copy(pattern_hbm, pattern, loaded.at[1])
    load_table.start()
    load_pattern.start()

    pairs = route.shape[1]
    slots = devices * capacity
    ia = lax.broadcasted_iota(jnp.int32, (pairs, pairs), 0)
    ib = lax.broadcasted_iota(jnp.int32, (pairs, pairs), 1)

    def column(row):
        return jnp.sum(jnp.where(ia == ib, row, 0.0), 1, keepdims=True)

    dest = route[...].astype(F32)
    dest_col = column(dest)
    rank = jnp.sum(jnp.where((dest_col == dest) & (ib < ia), 1.0, 0.0), 1, keepdims=True)
    slot_lane = lax.broadcasted_iota(jnp.int32, (pairs, LANES), 1).astype(F32)
    match = (dest_col * capacity + rank) == slot_lane
    source_col = column(source[...].astype(F32))
    cell_col = column((kind[...] * blocks + target[...] + 1).astype(F32))
    sphere_lane = lax.broadcasted_iota(jnp.int32, (pairs, spheres), 1).astype(F32)
    entries = [cell_col, source_col]
    for j in range(BLOCK):
        picked = sphere_lane == source_col * BLOCK + j
        for axis in range(3):
            entries.append(
                jnp.sum(jnp.where(picked, pos_v[axis : axis + 1, :], 0.0), 1, keepdims=True)
            )
    rows = [jnp.sum(jnp.where(match, entry, 0.0), 0, keepdims=True) for entry in entries]
    all_small[me] = jnp.concatenate(rows, 0)
    all_mie[me] = jnp.concatenate([mie[0], mie[1]], 1).astype(BF16)

    pl.semaphore_wait(barrier, len(partners))

    copies = []

    def start(origin, mask, step):
        slot = mask if step == len(bits) else mask + bits[step]
        slot = slot + chips if step == len(bits) else slot
        back = chips * step + mask
        for at, ref in ((0, all_small), (1, all_mie)):
            copy = pltpu.make_async_remote_copy(
                src_ref=ref.at[origin], dst_ref=ref.at[origin],
                send_sem=send.at[at, back], recv_sem=recv.at[at, slot],
                device_id={"sph": partners[step]}, device_id_type=MESH,
            )
            copy.start()
            copies.append(copy)

    def arrived(at, slot):
        ref = (all_small, all_mie)[at]
        pltpu.make_async_remote_copy(
            src_ref=ref.at[me], dst_ref=ref.at[me],
            send_sem=send.at[at, 0], recv_sem=recv.at[at, slot],
            device_id={"sph": other}, device_id_type=MESH,
        ).wait_recv()

    def low(mask):
        return mask & -mask

    def origin_of(mask):
        value = chip
        for bit in bits:
            if mask & bit:
                value = flip(value, bit)
        return value * 2 + core

    for step in range(len(bits) + 1):
        start(me, 0, step)

    def forward(mask):
        arrived(0, mask)
        arrived(1, mask)
        for step, bit in enumerate(bits):
            if bit < low(mask):
                start(origin_of(mask), mask, step)
        start(origin_of(mask), mask, len(bits))

    waits = sorted(range(1, chips), key=lambda mask: (bin(mask).count("1"), -mask))

    per = LANES // dirs
    lane = lax.broadcasted_iota(jnp.int32, (1, LANES), 1)
    group = lane // dirs
    k_rows = []
    dir_row = jnp.zeros((1, LANES), jnp.int32)
    for axis in range(3):
        k_rows.append(jnp.zeros((1, LANES), F32))
    for d in range(dirs):
        here = lane % dirs == d
        index = dir_s[d]
        dir_row = jnp.where(here, index, dir_row)
        for axis in range(3):
            k_rows[axis] = jnp.where(here, wave_s[axis, index], k_rows[axis])

    def block_of(j):
        order = jnp.zeros((1, LANES), jnp.int32)
        for g in range(per):
            order = jnp.where(group == g, ORDER[j][g], order)
        return order

    orders = [block_of(j) for j in range(BLOCK)]
    steps = blocks // per
    tiles = [(q, j) for q in range(steps) for j in range(BLOCK)]
    sphere_at = jnp.concatenate([(orders[j] + q * per) * BLOCK + j for q, j in tiles], 0)
    here = [jnp.zeros((len(tiles), LANES), F32) for _ in range(3)]
    for s in range(spheres):
        mine = sphere_at == s
        for axis in range(3):
            here[axis] = jnp.where(mine, pos_s[axis, s], here[axis])

    def phase_of(x, y, z):
        return sincos(x * k_rows[0] + y * k_rows[1] + z * k_rows[2])

    own_c, own_s = phase_of(*here)
    own_e[0] = own_c
    own_e[1] = own_s

    def prepare_table():
        load_table.wait()
        for c in range(0, classes, 2):
            at = pl.ds(c * modes, 2 * modes)
            real = jnp.concatenate([table[c, 0], table[c + 1, 0]], 1)
            imag = jnp.concatenate([table[c, 1], table[c + 1, 1]], 1)
            t_real[:, at] = real
            t_diff[:, at] = imag - real
            t_sum[:, at] = imag + real

    def prepare_field():
        load_pattern.wait()
        tables = pattern.shape[2]
        chosen = (lax.broadcasted_iota(jnp.int32, (tables, LANES), 0) == dir_row).astype(F32).astype(BF16)
        for p in range(2):
            high, rest = split_two(pattern[p])
            pat[p] = jnp.dot(high, chosen, preferred_element_type=F32) + jnp.dot(
                rest, chosen, preferred_element_type=F32
            )
        sphere_id = lax.broadcasted_iota(jnp.int32, (spheres, LANES), 0)
        picks = jnp.concatenate(
            [(sphere_id == sphere_at[t : t + 1]).astype(F32) for t in range(len(tiles))], 1
        )
        picks = jnp.concatenate([picks, picks], 0).astype(BF16)
        for p in range(2):
            pieces = jnp.concatenate(split_two(mie[p]), 0)
            spread[p] = lax.dot_general(
                pieces, picks, (((0,), (0,)), ((), ())), preferred_element_type=F32
            )
        for t in range(len(tiles)):
            at = pl.ds(t * LANES, LANES)
            c, s = own_c[t : t + 1], own_s[t : t + 1]
            inc[0, :, at] = c * pat[0] - s * pat[1]
            inc[1, :, at] = c * pat[1] + s * pat[0]

    for mask in waits[:1]:
        forward(mask)
    prepare_table()
    for mask in waits[1:3]:
        forward(mask)
    prepare_field()
    for mask in waits[3:]:
        forward(mask)
    for slot in range(chips):
        arrived(0, chips + slot)

    slot_id = lax.broadcasted_iota(jnp.int32, (slots, devices), 0)
    from_device = (slot_id // capacity == lax.broadcasted_iota(jnp.int32, (slots, devices), 1)).astype(F32)
    lists = jnp.concatenate([all_small[:, r, :] for r in range(8)], 1)
    lists = jnp.dot(from_device, lists, precision=HIGHEST, preferred_element_type=F32)
    slot_row = lax.broadcasted_iota(jnp.int32, (slots, LANES), 0)
    slot_lane = lax.broadcasted_iota(jnp.int32, (slots, LANES), 1)
    wanted = slot_lane == me * capacity + slot_row % capacity
    cols = [
        jnp.sum(jnp.where(wanted, lists[:, r * LANES : (r + 1) * LANES], 0.0), 1, keepdims=True)
        for r in range(8)
    ]
    cell = cols[0].astype(jnp.int32) - 1
    owner = lax.broadcasted_iota(jnp.int32, (slots, 1), 0) // capacity
    row_of = owner * spheres + cols[1].astype(jnp.int32) * BLOCK
    for j in range(BLOCK):
        c, s = phase_of(*cols[2 + 3 * j : 5 + 3 * j])
        phase[j, :slots, :] = c
        phase[j, slots:, :] = s
        delta[j] = cell - orders[j]
    total = devices * spheres
    at_row = lax.broadcasted_iota(jnp.int32, (slots, total), 1)
    pick = jnp.concatenate(
        [(at_row == row_of + j).astype(F32).astype(BF16) for j in range(BLOCK)], 0
    )

    for slot in range(chips):
        arrived(1, chips + slot)
    gathered = jnp.dot(
        pick, all_mie[...].reshape(total, 2 * modes), preferred_element_type=F32
    )
    for j in range(BLOCK):
        turned = gathered[j * slots : (j + 1) * slots].T.astype(BF16)
        real, imag = turned[:modes], turned[modes:]
        weights[j, :modes, :slots] = real
        weights[j, modes:, :slots] = imag
        weights[j, :modes, slots:] = -imag
        weights[j, modes:, slots:] = real

    width = BLOCK * LANES

    def step_body(q, carry):
        for j in range(BLOCK):
            c_all, s_all = phase[j, :slots, :], phase[j, slots:, :]
            for c in range(0, classes, 2):
                tops, bottoms = [], []
                for h in range(2):
                    here = delta[j] == (c + h) * blocks + q * per
                    tops.append(jnp.where(here, c_all, 0.0))
                    bottoms.append(jnp.where(here, s_all, 0.0))
                masked = jnp.concatenate(
                    [jnp.concatenate(tops, 1), jnp.concatenate(bottoms, 1)], 0
                ).astype(BF16)
                y_at[...] = jnp.dot(weights[j], masked, preferred_element_type=F32)
                for h in range(2):
                    at = pl.ds(h * LANES, LANES)
                    yr, yi = y_at[:modes, at], y_at[modes:, at]
                    pr, pi = pat[0], pat[1]
                    mr = yr * pr - yi * pi
                    mi = yr * pi + yi * pr
                    rows = pl.ds((c + h) * modes, modes)
                    lanes = pl.ds(j * LANES, LANES)
                    x_real[rows, lanes] = mr.astype(BF16)
                    x_imag[rows, lanes] = mi.astype(BF16)
                    x_sum[rows, lanes] = (mr + mi).astype(BF16)
        both = jnp.dot(t_real[...], x_sum[...], preferred_element_type=F32)
        first = jnp.dot(t_diff[...], x_real[...], preferred_element_type=F32)
        second = jnp.dot(t_sum[...], x_imag[...], preferred_element_type=F32)
        at = pl.ds(pl.multiple_of(q * width, width), width)
        inc_r, inc_i = inc[0, :, at], inc[1, :, at]
        total_r = inc_r + (both - second)
        total_i = inc_i + (both + first)
        mr, mi = spread[0, :, at], spread[1, :, at]
        out_r = mr * total_r - mi * total_i
        out_i = mr * total_i + mi * total_r
        terms = inc_r * out_r + inc_i * out_i
        terms = jnp.sum(terms.reshape(modes // 8, 8, width), 0)
        part[...] += terms[:, :LANES] + terms[:, LANES:]
        even = (lax.broadcasted_iota(jnp.int32, (modes, LANES), 1) // dirs) % 2 == 0
        for p, out in ((0, out_r), (1, out_i)):
            left, right = out[:, :LANES], out[:, LANES:]
            head = jnp.where(even, left, right)
            tail = pltpu.roll(jnp.where(even, right, left), LANES - dirs, 1)
            rows = pl.ds(p * modes, modes)
            out_at[q, rows, :LANES] = head.astype(BF16)
            out_at[q, rows, LANES:] = tail.astype(BF16)
        pltpu.make_async_copy(out_at.at[q], scattered.at[:, at], stored.at[q]).start()
        return carry

    part[...] = jnp.zeros_like(part)
    lax.fori_loop(0, steps, step_body, 0)

    row = jnp.sum(part[...], 0, keepdims=True)
    part[...] = jnp.broadcast_to(row, part.shape)
    sends = []
    for r, peer in enumerate(everyone):
        copy = pltpu.make_async_remote_copy(
            src_ref=part, dst_ref=inbox.at[me], send_sem=ext_send.at[r], recv_sem=ext_recv.at[r],
            device_id={"sph": peer}, device_id_type=MESH,
        )
        copy.start()
        sends.append(copy)
    inbox[me] = part[...]
    for copy in copies:
        copy.wait_send()
    for q in range(steps):
        at = pl.ds(q * width, width)
        pltpu.make_async_copy(out_at.at[q], scattered.at[:, at], stored.at[q]).wait()
    for copy in sends:
        copy.wait_recv()
    row = jnp.sum(inbox[...], 0)[:1]
    shift = LANES // 2
    while shift >= dirs:
        row = row + pltpu.roll(row, shift, 1)
        shift //= 2
    ext[...] = row
    for copy in sends:
        copy.wait_send()


def shards(
    positions, wave_vectors, pattern, dir_index, mie, trans_table, pair_route, pair_source,
    pair_target, pair_class,
):
    modes = pattern.shape[1]
    spheres = positions.shape[0]
    dirs = dir_index.shape[0]
    blocks = spheres // BLOCK
    classes = trans_table.shape[0]
    devices = lax.axis_size("sph")
    pair_count = pair_source.shape[0]
    capacity = max(2, 2 * pair_count // devices)
    slots = devices * capacity
    chips = devices // 2
    bits = chips.bit_length() - 1
    per = LANES // dirs
    steps = blocks // per
    width = BLOCK * LANES
    depth = classes * modes
    columns = steps * width
    assert chips == 1 << bits and slots == LANES and per == len(ORDER[0]) and BLOCK == len(ORDER)

    vmem = pl.BlockSpec(memory_space=pltpu.VMEM)
    smem = pl.BlockSpec(memory_space=pltpu.SMEM)
    anywhere = pl.BlockSpec(memory_space=pl.ANY)
    dims = (modes, dirs, spheres, blocks, classes, devices, capacity)
    dma = pltpu.SemaphoreType.DMA
    scattered, ext = pl.pallas_call(
        functools.partial(fused_kernel, dims),
        out_shape=[
            jax.ShapeDtypeStruct((2 * modes, columns), BF16),
            jax.ShapeDtypeStruct((1, LANES), F32),
        ],
        in_specs=[vmem] * 4 + [smem, vmem, smem, smem, vmem, anywhere, anywhere],
        out_specs=[anywhere, vmem],
        scratch_shapes=[
            pltpu.VMEM(trans_table.shape, BF16),
            pltpu.VMEM(pattern.shape, F32),
            pltpu.VMEM((modes, depth), BF16),
            pltpu.VMEM((modes, depth), BF16),
            pltpu.VMEM((modes, depth), BF16),
            pltpu.VMEM((devices, spheres, 2 * modes), BF16),
            pltpu.VMEM((devices, 8, LANES), F32),
            pltpu.VMEM((BLOCK, 2 * modes, 2 * slots), BF16),
            pltpu.VMEM((depth, width), BF16),
            pltpu.VMEM((depth, width), BF16),
            pltpu.VMEM((depth, width), BF16),
            pltpu.VMEM((2, modes, LANES), F32),
            pltpu.VMEM((2, modes, columns), F32),
            pltpu.VMEM((2, modes, columns), F32),
            pltpu.VMEM((2, steps * BLOCK, LANES), F32),
            pltpu.VMEM((BLOCK, 2 * slots, LANES), F32),
            pltpu.VMEM((BLOCK, slots, LANES), jnp.int32),
            pltpu.VMEM((2 * modes, width), F32),
            pltpu.VMEM((steps, 2 * modes, width), BF16),
            pltpu.VMEM((8, LANES), F32),
            pltpu.VMEM((devices, 8, LANES), F32),
            dma((2,)),
            dma((steps,)),
            dma((2, chips * (bits + 1))),
            dma((2, 2 * chips)),
            dma((devices,)),
            dma((devices,)),
        ],
        compiler_params=pltpu.CompilerParams(
            collective_id=0, has_side_effects=True, vmem_limit_bytes=63 * 1024 * 1024
        ),
        name="fused",
    )(
        pair_route.reshape(1, pair_count), pair_source.reshape(1, pair_count),
        pair_target.reshape(1, pair_count), pair_class.reshape(1, pair_count),
        positions.T, positions.T, wave_vectors.T, dir_index, jnp.transpose(mie, (0, 2, 1)),
        pattern, trans_table,
    )
    return scattered, ext[0, :dirs]


def solution(mesh):
    placed = (
        P("sph", None), P(), P(), P("groups"), P(None, None, "sph"), P(),
        P("sph", None), P("sph"), P("sph"), P("sph"),
    )
    return jax.shard_map(
        shards,
        mesh=mesh,
        in_specs=placed,
        out_specs=(P(None, ("groups", "sph")), P("groups")),
        check_vma=False,
    )
```

time: 95 us -> 50.7 us (0.53)
  Pallas kernels: 74.6 us -> 45.8 us
  other arithmetic: 7.1 us -> 0 us
  local copies, waits for them, and re-layouts: 7.9 us -> 4.05 us
  matrix products: 3.56 us -> 0 us
    pallas_call x3 -> x1, Pallas kernels: 74.6 us -> 45.8 us  [shards(): pl.pallas_call(functools.partial(fused_kernel, dims), out_shape=[jax.Shap...]
    dot_general x3 -> x0, matrix products: 3.56 us -> none  [the longest x1 1.46 us: shards(): jnp.einsum('cmt,td->cmd', pattern, select_tile, precision=HIGHEST)]
    mul x17 -> x0, local copies, waits for them, and re-layouts: 1.84 us -> none  [the longest x7 1.17 us: shards(): positions[:, 0:1] * k[None, :, 0] + positions[:, 1:2] * k[None, :, 1]]
    eq x3 -> x0, other arithmetic: 1.42 us -> none  [the longest x2 0.74 us: shards(): match = slot_of[:, None] == jnp.arange(slots, dtype=jnp.int32)[None, :]]
    convert_element_type x2 -> x0, other arithmetic: 1.42 us -> none  [the longest x1 0.73 us: shards(): lists = (lists - jnp.array([[1], [0], [0]], jnp.int32)).astype(jnp.float32)]
    concatenate x2 -> x0, other arithmetic: 1.4 us -> none  [the longest x1 0.73 us: shards(): jnp.concatenate([pat_rows] * BLOCK, 1)]
    reduce_sum x2 -> x0, other arithmetic: 1.04 us -> none  [the longest x1 0.93 us: shards(): jnp.sum(((dest[:, None] == dest[None, :]) & (order[None, :] < order[:, No...]
    unnamed x5 -> x1, local copies, waits for them, and re-layouts: 2.58 us -> 2.87 us
where the time goes in v1:
time: 50.7 us; the launch traced here: 50.5 us
  Pallas kernels  45.8 us (90%)
  local copies, waits for them, and re-layouts  4.05 us (8%)
  between operations  0.64 us (1%)
    pallas_call x1, Pallas kernels, shards(): pl.pallas_call(functools.partial(fused_kernel, dims), out_shape=[jax.Shap...  45.8 us
    unnamed x1, local copies, waits for them, and re-layouts  2.87 us
    squeeze x1, local copies, waits for them, and re-layouts, shards(): return (scattered, ext[0, :dirs])  1.18 us

profile of v1, /device:TPU:0, one launch (start us, length us, event | category | flops | bytes accessed | tf_op | source)
XLA Modules:
  0.0 50.5 jit_solution(6736109221612510548)
XLA Ops:
  0.6 45.8 %fused.1 = (bf16[896,1024]{1,0:T(8,128)(2,1)}, f32[1,128]{1,0:T(1,128)}) custom-call(s32[1,64]{1,0:T(1,128)} %bitcast.13, s32[1,64]{1,0:T(1,128)} %bitcast.14, s32[1,64]{1,0:T(1,128)} %bitcast.15, s32[1,64]{1,0:T(1,128)} %bitcast.16, f32[3,32]{1,0:T(4,128)} %bitcast.10, f32[3,32]{1,0:T(4,128)} %bitcast.11, f32[3,256]{1,0:T(4,128)} %bitcast.12, s32[32]{0:T(128)} %dir_s.1, ...), custom_call_target="tpu_custom_call" | custom-call | tf_op jit(solution)/shard_map/fused/pallas_call | solution.py:381
  46.4 1.2 %slice_bitcast_fusion = f32[32]{0:T(128)} fusion(f32[1,128]{1,0:T(1,128)} %get-tuple-element.5), kind=kLoop, calls=%fused_computation | loop fusion | bytes 256 | tf_op jit(solution)/shard_map/squeeze | solution.py:428
  47.6 2.9 %copy.13 = bf16[896,1024]{1,0:T(8,128)(2,1)} copy(bf16[896,1024]{1,0:T(8,128)(2,1)} %get-tuple-element.8) | data formatting | bytes 3670016

commit v2 on v1

--- a/solution.py
+++ b/solution.py
@@ -14,6 +14,8 @@
 F32 = jnp.float32
 BF16 = jnp.bfloat16
 ORDER = ((0, 2, 1, 3), (3, 0, 2, 1))
+PARTS = 4
+DEPTH = 512
 
 
 def sincos(angle):
@@ -46,10 +48,11 @@
     dims, route, source, target, kind, pos_s, pos_v, wave_s, dir_s, mie, pattern_hbm, table_hbm,
     scattered, ext,
     table, pattern, t_real, t_diff, t_sum, all_mie, all_small, weights, x_real, x_imag, x_sum,
-    pat, inc, spread, own_e, phase, delta, y_at, out_at, part, inbox,
+    pat, inc, spread, own_e, phase, delta, out_at, part, inbox,
     loaded, stored, send, recv, ext_send, ext_recv,
 ):
     modes, dirs, spheres, blocks, classes, devices, capacity = dims
+    chunk = modes // PARTS
     me = lax.axis_index("sph")
     chips = devices // 2
     chip, core = me // 2, me % 2
@@ -265,14 +268,19 @@
     for j in range(BLOCK):
         turned = gathered[j * slots : (j + 1) * slots].T.astype(BF16)
         real, imag = turned[:modes], turned[modes:]
-        weights[j, :modes, :slots] = real
-        weights[j, modes:, :slots] = imag
-        weights[j, :modes, slots:] = -imag
-        weights[j, modes:, slots:] = real
+        for g in range(PARTS):
+            piece = slice(g * chunk, (g + 1) * chunk)
+            upper = pl.ds(2 * g * chunk, chunk)
+            lower = pl.ds((2 * g + 1) * chunk, chunk)
+            weights[j, upper, :slots] = real[piece]
+            weights[j, upper, slots:] = -imag[piece]
+            weights[j, lower, :slots] = imag[piece]
+            weights[j, lower, slots:] = real[piece]
 
     width = BLOCK * LANES
 
-    def step_body(q, carry):
+    def build(q):
+        work = []
         for j in range(BLOCK):
             c_all, s_all = phase[j, :slots, :], phase[j, slots:, :]
             for c in range(0, classes, 2):
@@ -284,22 +292,28 @@
                 masked = jnp.concatenate(
                     [jnp.concatenate(tops, 1), jnp.concatenate(bottoms, 1)], 0
                 ).astype(BF16)
-                y_at[...] = jnp.dot(weights[j], masked, preferred_element_type=F32)
-                for h in range(2):
-                    at = pl.ds(h * LANES, LANES)
-                    yr, yi = y_at[:modes, at], y_at[modes:, at]
-                    pr, pi = pat[0], pat[1]
-                    mr = yr * pr - yi * pi
-                    mi = yr * pi + yi * pr
-                    rows = pl.ds((c + h) * modes, modes)
-                    lanes = pl.ds(j * LANES, LANES)
-                    x_real[rows, lanes] = mr.astype(BF16)
-                    x_imag[rows, lanes] = mi.astype(BF16)
-                    x_sum[rows, lanes] = (mr + mi).astype(BF16)
-        both = jnp.dot(t_real[...], x_sum[...], preferred_element_type=F32)
-        first = jnp.dot(t_diff[...], x_real[...], preferred_element_type=F32)
-        second = jnp.dot(t_sum[...], x_imag[...], preferred_element_type=F32)
-        at = pl.ds(pl.multiple_of(q * width, width), width)
+                for g in range(PARTS):
+                    work.append(functools.partial(piece_of, q, j, c, g, masked))
+        return work
+
+    def piece_of(q, j, c, g, masked):
+        both = pl.ds(2 * g * chunk, 2 * chunk)
+        y = jnp.dot(weights[j, both, :], masked, preferred_element_type=F32)
+        own = pl.ds(g * chunk, chunk)
+        pr, pi = pat[0, own, :], pat[1, own, :]
+        for h in range(2):
+            at = slice(h * LANES, (h + 1) * LANES)
+            yr, yi = y[:chunk, at], y[chunk:, at]
+            mr = yr * pr - yi * pi
+            mi = yr * pi + yi * pr
+            rows = pl.ds((c + h) * modes + g * chunk, chunk)
+            lanes = pl.ds(j * LANES, LANES)
+            x_real[q, rows, lanes] = mr.astype(BF16)
+            x_imag[q, rows, lanes] = mi.astype(BF16)
+            x_sum[q, rows, lanes] = (mr + mi).astype(BF16)
+
+    def finish(q, both, first, second):
+        at = pl.ds(q * width, width)
         inc_r, inc_i = inc[0, :, at], inc[1, :, at]
         total_r = inc_r + (both - second)
         total_i = inc_i + (both + first)
@@ -317,23 +331,42 @@
             rows = pl.ds(p * modes, modes)
             out_at[q, rows, :LANES] = head.astype(BF16)
             out_at[q, rows, LANES:] = tail.astype(BF16)
+
+    part[...] = jnp.zeros_like(part)
+    for work in build(0):
+        work()
+    pairs_of = ((t_real, x_sum), (t_diff, x_real), (t_sum, x_imag))
+    deep = classes * modes // DEPTH
+    for q in range(steps):
+        todo = build(q + 1) if q + 1 < steps else []
+        done = 0
+        results = []
+        for n, (matrix, mixed) in enumerate(pairs_of):
+            value = None
+            for i in range(deep):
+                at = slice(i * DEPTH, (i + 1) * DEPTH)
+                term = jnp.dot(matrix[:, at], mixed[q, at, :], preferred_element_type=F32)
+                value = term if value is None else value + term
+                while done < (n * deep + i + 1) * len(todo) // (3 * deep):
+                    todo[done]()
+                    done += 1
+            results.append(value)
+        finish(q, *results)
+
+    for q in range(steps):
+        at = pl.ds(q * width, width)
         pltpu.make_async_copy(out_at.at[q], scattered.at[:, at], stored.at[q]).start()
-        return carry
-
-    part[...] = jnp.zeros_like(part)
-    lax.fori_loop(0, steps, step_body, 0)
-
     row = jnp.sum(part[...], 0, keepdims=True)
-    part[...] = jnp.broadcast_to(row, part.shape)
+    part[0:1, :] = row
     sends = []
     for r, peer in enumerate(everyone):
         copy = pltpu.make_async_remote_copy(
-            src_ref=part, dst_ref=inbox.at[me], send_sem=ext_send.at[r], recv_sem=ext_recv.at[r],
+            src_ref=part.at[pl.ds(0, 1)], dst_ref=inbox.at[me], send_sem=ext_send.at[r], recv_sem=ext_recv.at[r],
             device_id={"sph": peer}, device_id_type=MESH,
         )
         copy.start()
         sends.append(copy)
-    inbox[me] = part[...]
+    inbox[me] = row
     for copy in copies:
         copy.wait_send()
     for q in range(steps):
@@ -341,7 +374,7 @@
         pltpu.make_async_copy(out_at.at[q], scattered.at[:, at], stored.at[q]).wait()
     for copy in sends:
         copy.wait_recv()
-    row = jnp.sum(inbox[...], 0)[:1]
+    row = jnp.sum(inbox[...], 0)
     shift = LANES // 2
     while shift >= dirs:
         row = row + pltpu.roll(row, shift, 1)
@@ -371,6 +404,7 @@
     width = BLOCK * LANES
     depth = classes * modes
     columns = steps * width
+    assert modes % (16 * PARTS) == 0 and depth % DEPTH == 0 and classes % 2 == 0
     assert chips == 1 << bits and slots == LANES and per == len(ORDER[0]) and BLOCK == len(ORDER)
 
     vmem = pl.BlockSpec(memory_space=pltpu.VMEM)
@@ -395,19 +429,18 @@
             pltpu.VMEM((devices, spheres, 2 * modes), BF16),
             pltpu.VMEM((devices, 8, LANES), F32),
             pltpu.VMEM((BLOCK, 2 * modes, 2 * slots), BF16),
-            pltpu.VMEM((depth, width), BF16),
-            pltpu.VMEM((depth, width), BF16),
-            pltpu.VMEM((depth, width), BF16),
+            pltpu.VMEM((steps, depth, width), BF16),
+            pltpu.VMEM((steps, depth, width), BF16),
+            pltpu.VMEM((steps, depth, width), BF16),
             pltpu.VMEM((2, modes, LANES), F32),
             pltpu.VMEM((2, modes, columns), F32),
             pltpu.VMEM((2, modes, columns), F32),
             pltpu.VMEM((2, steps * BLOCK, LANES), F32),
             pltpu.VMEM((BLOCK, 2 * slots, LANES), F32),
             pltpu.VMEM((BLOCK, slots, LANES), jnp.int32),
-            pltpu.VMEM((2 * modes, width), F32),
             pltpu.VMEM((steps, 2 * modes, width), BF16),
             pltpu.VMEM((8, LANES), F32),
-            pltpu.VMEM((devices, 8, LANES), F32),
+            pltpu.VMEM((devices, 1, LANES), F32),
             dma((2,)),
             dma((steps,)),
             dma((2, chips * (bits + 1))),

time: 50.7 us -> 45.7 us (0.901)
  Pallas kernels: 45.8 us -> 40.8 us
    pallas_call x1, Pallas kernels: 45.8 us -> 40.8 us  [shards(): pl.pallas_call(functools.partial(fused_kernel, dims), out_shape=[jax.Shap...]
where the time goes in v2:
time: 45.7 us; the launch traced here: 45.5 us
  Pallas kernels  40.8 us (89%)
  local copies, waits for them, and re-layouts  4.05 us (9%)
  between operations  0.64 us (1%)
    pallas_call x1, Pallas kernels, shards(): pl.pallas_call(functools.partial(fused_kernel, dims), out_shape=[jax.Shap...  40.8 us
    unnamed x1, local copies, waits for them, and re-layouts  2.87 us
    squeeze x1, local copies, waits for them, and re-layouts, shards(): return (scattered, ext[0, :dirs])  1.18 us

profile of v2, /device:TPU:0, one launch (start us, length us, event | category | flops | bytes accessed | tf_op | source)
XLA Modules:
  0.0 45.5 jit_solution(18372165985695632021)
XLA Ops:
  0.6 40.8 %fused.1 = (bf16[896,1024]{1,0:T(8,128)(2,1)}, f32[1,128]{1,0:T(1,128)}) custom-call(s32[1,64]{1,0:T(1,128)} %bitcast.13, s32[1,64]{1,0:T(1,128)} %bitcast.14, s32[1,64]{1,0:T(1,128)} %bitcast.15, s32[1,64]{1,0:T(1,128)} %bitcast.16, f32[3,32]{1,0:T(4,128)} %bitcast.10, f32[3,32]{1,0:T(4,128)} %bitcast.11, f32[3,256]{1,0:T(4,128)} %bitcast.12, s32[32]{0:T(128)} %dir_s.1, ...), custom_call_target="tpu_custom_call" | custom-call | tf_op jit(solution)/shard_map/fused/pallas_call | solution.py:415
  41.4 1.2 %slice_bitcast_fusion = f32[32]{0:T(128)} fusion(f32[1,128]{1,0:T(1,128)} %get-tuple-element.5), kind=kLoop, calls=%fused_computation | loop fusion | bytes 256 | tf_op jit(solution)/shard_map/squeeze | solution.py:461
  42.6 2.9 %copy.13 = bf16[896,1024]{1,0:T(8,128)(2,1)} copy(bf16[896,1024]{1,0:T(8,128)(2,1)} %get-tuple-element.8) | data formatting | bytes 3670016

commit v3 on v2

--- a/solution.py
+++ b/solution.py
@@ -45,11 +45,11 @@
 
 
 def fused_kernel(
-    dims, route, source, target, kind, pos_s, pos_v, wave_s, dir_s, mie, pattern_hbm, table_hbm,
-    scattered, ext,
-    table, pattern, t_real, t_diff, t_sum, all_mie, all_small, weights, x_real, x_imag, x_sum,
-    pat, inc, spread, own_e, phase, delta, out_at, part, inbox,
-    loaded, stored, send, recv, ext_send, ext_recv,
+    dims, route_hbm, source_hbm, target_hbm, kind_hbm, pos_hbm, wave_hbm, dir_hbm, mie_hbm,
+    pattern_hbm, table_hbm, scattered, ext,
+    route, source, target, kind, pos_s, pos_v, wave_s, dir_s, mie, table, pattern, t_real, t_diff, t_sum, all_mie, all_small, weights, x_real, x_imag, x_sum,
+    pat, inc, spread, own_e, phase, delta, part, inbox,
+    loaded, send, recv, ext_send, ext_recv,
 ):
     modes, dirs, spheres, blocks, classes, devices, capacity = dims
     chunk = modes // PARTS
@@ -66,7 +66,25 @@
     def flip(value, bit):
         return value + bit - 2 * bit * ((value // bit) % 2)
 
-    partners = [flip(chip, bit) * 2 + core for bit in bits] + [other]
+    def chip_at(mask):
+        value = chip
+        for bit in bits:
+            if mask & bit:
+                value = flip(value, bit)
+        return value
+
+    stages = [[bit] for bit in bits[:-2]] + [bits[-2:] + [sum(bits[-2:])] if len(bits) > 1 else bits]
+    held, routes = [0], []
+    for stage, offsets in enumerate(stages):
+        routes.append((list(held), offsets))
+        held = held + [h | o for o in offsets for h in held]
+    stage_of = {0: -1}
+    for stage, (before, offsets) in enumerate(routes):
+        for o in offsets:
+            for h in before:
+                stage_of[h | o] = stage
+    greeted = [o for offsets in stages for o in offsets]
+    partners = [chip_at(o) * 2 + core for o in greeted] + [other]
     everyone = [(me + r) % devices for r in range(1, devices)]
 
     barrier = pltpu.get_barrier_semaphore()
@@ -74,8 +92,17 @@
         pl.semaphore_signal(barrier, inc=1, device_id={"sph": peer}, device_id_type=MESH)
     load_table = pltpu.make_async_copy(table_hbm, table, loaded.at[0])
     load_pattern = pltpu.make_async_copy(pattern_hbm, pattern, loaded.at[1])
+    small = (
+        (route_hbm, route), (source_hbm, source), (target_hbm, target), (kind_hbm, kind),
+        (pos_hbm, pos_v), (mie_hbm, mie), (pos_hbm, pos_s), (wave_hbm, wave_s), (dir_hbm, dir_s),
+    )
+    fetches = [pltpu.make_async_copy(a, b, loaded.at[2 + i]) for i, (a, b) in enumerate(small)]
+    for copy in fetches:
+        copy.start()
+    load_pattern.start()
     load_table.start()
-    load_pattern.start()
+    for copy in fetches:
+        copy.wait()
 
     pairs = route.shape[1]
     slots = devices * capacity
@@ -107,50 +134,39 @@
     pl.semaphore_wait(barrier, len(partners))
 
     copies = []
-
-    def start(origin, mask, step):
-        slot = mask if step == len(bits) else mask + bits[step]
-        slot = slot + chips if step == len(bits) else slot
-        back = chips * step + mask
-        for at, ref in ((0, all_small), (1, all_mie)):
-            copy = pltpu.make_async_remote_copy(
-                src_ref=ref.at[origin], dst_ref=ref.at[origin],
-                send_sem=send.at[at, back], recv_sem=recv.at[at, slot],
-                device_id={"sph": partners[step]}, device_id_type=MESH,
-            )
-            copy.start()
-            copies.append(copy)
+    items = (all_small, all_mie)
+
+    def start(at, mask, offset):
+        ref = items[at].at[chip_at(mask) * 2 + core]
+        slot = chips + mask if offset is None else mask | offset
+        target = other if offset is None else chip_at(offset) * 2 + core
+        copy = pltpu.make_async_remote_copy(
+            src_ref=ref, dst_ref=ref, send_sem=send.at[at, len(copies) // 2],
+            recv_sem=recv.at[at, slot], device_id={"sph": target}, device_id_type=MESH,
+        )
+        copy.start()
+        copies.append(copy)
 
     def arrived(at, slot):
-        ref = (all_small, all_mie)[at]
+        ref = items[at].at[me]
         pltpu.make_async_remote_copy(
-            src_ref=ref.at[me], dst_ref=ref.at[me],
-            send_sem=send.at[at, 0], recv_sem=recv.at[at, slot],
+            src_ref=ref, dst_ref=ref, send_sem=send.at[at, 0], recv_sem=recv.at[at, slot],
             device_id={"sph": other}, device_id_type=MESH,
         ).wait_recv()
 
-    def low(mask):
-        return mask & -mask
-
-    def origin_of(mask):
-        value = chip
-        for bit in bits:
-            if mask & bit:
-                value = flip(value, bit)
-        return value * 2 + core
-
-    for step in range(len(bits) + 1):
-        start(me, 0, step)
+    def hand_on(mask):
+        later = [o for offsets in stages[stage_of[mask] + 1 :] for o in offsets]
+        for offset in later + [None]:
+            for at in range(2):
+                start(at, mask, offset)
 
     def forward(mask):
-        arrived(0, mask)
-        arrived(1, mask)
-        for step, bit in enumerate(bits):
-            if bit < low(mask):
-                start(origin_of(mask), mask, step)
-        start(origin_of(mask), mask, len(bits))
-
-    waits = sorted(range(1, chips), key=lambda mask: (bin(mask).count("1"), -mask))
+        for at in range(2):
+            arrived(at, mask)
+        hand_on(mask)
+
+    hand_on(0)
+    waits = sorted(range(1, chips), key=lambda m: (bin(m).count("1"), -m))
 
     per = LANES // dirs
     lane = lax.broadcasted_iota(jnp.int32, (1, LANES), 1)
@@ -224,14 +240,14 @@
             inc[0, :, at] = c * pat[0] - s * pat[1]
             inc[1, :, at] = c * pat[1] + s * pat[0]
 
-    for mask in waits[:1]:
-        forward(mask)
     prepare_table()
-    for mask in waits[1:3]:
+    early = [m for m in waits if m in greeted][:3]
+    for mask in early:
         forward(mask)
     prepare_field()
-    for mask in waits[3:]:
-        forward(mask)
+    for mask in waits:
+        if mask not in early:
+            forward(mask)
     for slot in range(chips):
         arrived(0, chips + slot)
 
@@ -308,9 +324,9 @@
             mi = yr * pi + yi * pr
             rows = pl.ds((c + h) * modes + g * chunk, chunk)
             lanes = pl.ds(j * LANES, LANES)
-            x_real[q, rows, lanes] = mr.astype(BF16)
-            x_imag[q, rows, lanes] = mi.astype(BF16)
-            x_sum[q, rows, lanes] = (mr + mi).astype(BF16)
+            x_real[q % 2, rows, lanes] = mr.astype(BF16)
+            x_imag[q % 2, rows, lanes] = mi.astype(BF16)
+            x_sum[q % 2, rows, lanes] = (mr + mi).astype(BF16)
 
     def finish(q, both, first, second):
         at = pl.ds(q * width, width)
@@ -329,8 +345,8 @@
             head = jnp.where(even, left, right)
             tail = pltpu.roll(jnp.where(even, right, left), LANES - dirs, 1)
             rows = pl.ds(p * modes, modes)
-            out_at[q, rows, :LANES] = head.astype(BF16)
-            out_at[q, rows, LANES:] = tail.astype(BF16)
+            scattered[rows, pl.ds(q * width, LANES)] = head.astype(BF16)
+            scattered[rows, pl.ds(q * width + LANES, LANES)] = tail.astype(BF16)
 
     part[...] = jnp.zeros_like(part)
     for work in build(0):
@@ -345,7 +361,7 @@
             value = None
             for i in range(deep):
                 at = slice(i * DEPTH, (i + 1) * DEPTH)
-                term = jnp.dot(matrix[:, at], mixed[q, at, :], preferred_element_type=F32)
+                term = jnp.dot(matrix[:, at], mixed[q % 2, at, :], preferred_element_type=F32)
                 value = term if value is None else value + term
                 while done < (n * deep + i + 1) * len(todo) // (3 * deep):
                     todo[done]()
@@ -353,9 +369,6 @@
             results.append(value)
         finish(q, *results)
 
-    for q in range(steps):
-        at = pl.ds(q * width, width)
-        pltpu.make_async_copy(out_at.at[q], scattered.at[:, at], stored.at[q]).start()
     row = jnp.sum(part[...], 0, keepdims=True)
     part[0:1, :] = row
     sends = []
@@ -369,9 +382,6 @@
     inbox[me] = row
     for copy in copies:
         copy.wait_send()
-    for q in range(steps):
-        at = pl.ds(q * width, width)
-        pltpu.make_async_copy(out_at.at[q], scattered.at[:, at], stored.at[q]).wait()
     for copy in sends:
         copy.wait_recv()
     row = jnp.sum(inbox[...], 0)
@@ -408,8 +418,6 @@
     assert chips == 1 << bits and slots == LANES and per == len(ORDER[0]) and BLOCK == len(ORDER)
 
     vmem = pl.BlockSpec(memory_space=pltpu.VMEM)
-    smem = pl.BlockSpec(memory_space=pltpu.SMEM)
-    anywhere = pl.BlockSpec(memory_space=pl.ANY)
     dims = (modes, dirs, spheres, blocks, classes, devices, capacity)
     dma = pltpu.SemaphoreType.DMA
     scattered, ext = pl.pallas_call(
@@ -418,9 +426,18 @@
             jax.ShapeDtypeStruct((2 * modes, columns), BF16),
             jax.ShapeDtypeStruct((1, LANES), F32),
         ],
-        in_specs=[vmem] * 4 + [smem, vmem, smem, smem, vmem, anywhere, anywhere],
-        out_specs=[anywhere, vmem],
+        in_specs=[pl.BlockSpec(memory_space=pltpu.HBM)] * 10,
+        out_specs=[vmem, vmem],
         scratch_shapes=[
+            pltpu.VMEM((1, pair_count), jnp.int32),
+            pltpu.VMEM((1, pair_count), jnp.int32),
+            pltpu.VMEM((1, pair_count), jnp.int32),
+            pltpu.VMEM((1, pair_count), jnp.int32),
+            pltpu.SMEM((3, spheres), F32),
+            pltpu.VMEM((3, spheres), F32),
+            pltpu.SMEM((3, wave_vectors.shape[0]), F32),
+            pltpu.SMEM((dirs,), jnp.int32),
+            pltpu.VMEM((2, spheres, modes), F32),
             pltpu.VMEM(trans_table.shape, BF16),
             pltpu.VMEM(pattern.shape, F32),
             pltpu.VMEM((modes, depth), BF16),
@@ -429,34 +446,34 @@
             pltpu.VMEM((devices, spheres, 2 * modes), BF16),
             pltpu.VMEM((devices, 8, LANES), F32),
             pltpu.VMEM((BLOCK, 2 * modes, 2 * slots), BF16),
-            pltpu.VMEM((steps, depth, width), BF16),
-            pltpu.VMEM((steps, depth, width), BF16),
-            pltpu.VMEM((steps, depth, width), BF16),
+            pltpu.VMEM((2, depth, width), BF16),
+            pltpu.VMEM((2, depth, width), BF16),
+            pltpu.VMEM((2, depth, width), BF16),
             pltpu.VMEM((2, modes, LANES), F32),
             pltpu.VMEM((2, modes, columns), F32),
             pltpu.VMEM((2, modes, columns), F32),
             pltpu.VMEM((2, steps * BLOCK, LANES), F32),
             pltpu.VMEM((BLOCK, 2 * slots, LANES), F32),
             pltpu.VMEM((BLOCK, slots, LANES), jnp.int32),
-            pltpu.VMEM((steps, 2 * modes, width), BF16),
             pltpu.VMEM((8, LANES), F32),
             pltpu.VMEM((devices, 1, LANES), F32),
-            dma((2,)),
-            dma((steps,)),
-            dma((2, chips * (bits + 1))),
+            dma((11,)),
+            dma((2, 2 * chips)),
             dma((2, 2 * chips)),
             dma((devices,)),
             dma((devices,)),
         ],
         compiler_params=pltpu.CompilerParams(
-            collective_id=0, has_side_effects=True, vmem_limit_bytes=63 * 1024 * 1024
+            collective_id=0, has_side_effects=True, vmem_limit_bytes=48 * 1024 * 1024
         ),
         name="fused",
     )(
+        *[pltpu.with_memory_space_constraint(x, pltpu.HBM) for x in (
         pair_route.reshape(1, pair_count), pair_source.reshape(1, pair_count),
         pair_target.reshape(1, pair_count), pair_class.reshape(1, pair_count),
-        positions.T, positions.T, wave_vectors.T, dir_index, jnp.transpose(mie, (0, 2, 1)),
+        positions.T, wave_vectors.T, dir_index, jnp.transpose(mie, (0, 2, 1)),
         pattern, trans_table,
+        )]
     )
     return scattered, ext[0, :dirs]
 

time: 45.7 us -> 39.7 us (0.87)
  Pallas kernels: 40.8 us -> 37.1 us
  local copies, waits for them, and re-layouts: 4.05 us -> 1.74 us
    pallas_call x1, Pallas kernels: 40.8 us -> 37.1 us  [shards(): pl.pallas_call(functools.partial(fused_kernel, dims), out_shape=[jax.Shap...]
    unnamed x1, local copies, waits for them, and re-layouts: 2.87 us -> 1.23 us
    squeeze x1, local copies, waits for them, and re-layouts: 1.18 us -> 0.51 us  [shards(): return (scattered, ext[0, :dirs])]
where the time goes in v3:
time: 39.7 us; the launch traced here: 39.5 us
  Pallas kernels  37.1 us (93%)
  local copies, waits for them, and re-layouts  1.74 us (4%)
  between operations  0.64 us (2%)
    pallas_call x1, Pallas kernels, shards(): pl.pallas_call(functools.partial(fused_kernel, dims), out_shape=[jax.Shap...  37.1 us
    unnamed x1, local copies, waits for them, and re-layouts  1.23 us

profile of v3, /device:TPU:0, one launch (start us, length us, event | category | flops | bytes accessed | tf_op | source)
XLA Modules:
  0.0 39.5 jit_solution(1188827084846460405)
XLA Ops:
  0.6 37.1 %fused.1 = (bf16[896,1024]{1,0:T(8,128)(2,1)S(1)}, f32[1,128]{1,0:T(1,128)S(1)}) custom-call(s32[1,64]{1,0:T(1,128)} %bitcast.12, s32[1,64]{1,0:T(1,128)} %bitcast.13, s32[1,64]{1,0:T(1,128)} %bitcast.14, s32[1,64]{1,0:T(1,128)} %bitcast.15, f32[3,32]{1,0:T(4,128)} %bitcast.11, f32[3,256]{1,0:T(4,128)} %bitcast.10, s32[32]{0:T(128)} %dir_hbm.1, ...), custom_call_target="tpu_custom_call" | custom-call | tf_op jit(solution)/shard_map/fused/pallas_call | solution.py:423
  37.8 0.5 %slice_bitcast_fusion = f32[32]{0:T(128)} fusion(f32[1,128]{1,0:T(1,128)S(1)} %get-tuple-element.5), kind=kLoop, calls=%fused_computation | loop fusion | bytes 256 | tf_op jit(solution)/shard_map/squeeze | solution.py:478
  38.3 1.2 %copy.13 = bf16[896,1024]{1,0:T(8,128)(2,1)} copy(bf16[896,1024]{1,0:T(8,128)(2,1)S(1)} %get-tuple-element.8) | data formatting | bytes 3670016

commit v4 on v3

--- a/solution.py
+++ b/solution.py
@@ -16,6 +16,7 @@
 ORDER = ((0, 2, 1, 3), (3, 0, 2, 1))
 PARTS = 4
 DEPTH = 512
+SPLIT = 2
 
 
 def sincos(angle):
@@ -133,7 +134,7 @@
 
     pl.semaphore_wait(barrier, len(partners))
 
-    copies = []
+    copies = ([], [])
     items = (all_small, all_mie)
 
     def start(at, mask, offset):
@@ -141,11 +142,11 @@
         slot = chips + mask if offset is None else mask | offset
         target = other if offset is None else chip_at(offset) * 2 + core
         copy = pltpu.make_async_remote_copy(
-            src_ref=ref, dst_ref=ref, send_sem=send.at[at, len(copies) // 2],
+            src_ref=ref, dst_ref=ref, send_sem=send.at[at, len(copies[at])],
             recv_sem=recv.at[at, slot], device_id={"sph": target}, device_id_type=MESH,
         )
         copy.start()
-        copies.append(copy)
+        copies[at].append(copy)
 
     def arrived(at, slot):
         ref = items[at].at[me]
@@ -154,19 +155,22 @@
             device_id={"sph": other}, device_id_type=MESH,
         ).wait_recv()
 
-    def hand_on(mask):
+    def hand_on(at, mask):
         later = [o for offsets in stages[stage_of[mask] + 1 :] for o in offsets]
         for offset in later + [None]:
-            for at in range(2):
-                start(at, mask, offset)
-
-    def forward(mask):
-        for at in range(2):
+            start(at, mask, offset)
+
+    def forward(at, masks):
+        for mask in masks:
             arrived(at, mask)
-        hand_on(mask)
-
-    hand_on(0)
+            hand_on(at, mask)
+
+    hand_on(0, 0)
+    hand_on(1, 0)
     waits = sorted(range(1, chips), key=lambda m: (bin(m).count("1"), -m))
+    far = waits[:1]
+    near = [mask for mask in waits if mask in greeted and mask not in far]
+    relayed = [mask for mask in waits if mask not in greeted]
 
     per = LANES // dirs
     lane = lax.broadcasted_iota(jnp.int32, (1, LANES), 1)
@@ -240,14 +244,13 @@
             inc[0, :, at] = c * pat[0] - s * pat[1]
             inc[1, :, at] = c * pat[1] + s * pat[0]
 
+    forward(0, far)
+    forward(1, far)
     prepare_table()
-    early = [m for m in waits if m in greeted][:3]
-    for mask in early:
-        forward(mask)
+    forward(0, near + relayed)
+    forward(1, near)
     prepare_field()
-    for mask in waits:
-        if mask not in early:
-            forward(mask)
+    forward(1, relayed)
     for slot in range(chips):
         arrived(0, chips + slot)
 
@@ -297,9 +300,9 @@
 
     def build(q):
         work = []
-        for j in range(BLOCK):
-            c_all, s_all = phase[j, :slots, :], phase[j, slots:, :]
-            for c in range(0, classes, 2):
+        for c in range(0, classes, 2):
+            for j in range(BLOCK):
+                c_all, s_all = phase[j, :slots, :], phase[j, slots:, :]
                 tops, bottoms = [], []
                 for h in range(2):
                     here = delta[j] == (c + h) * blocks + q * per
@@ -328,46 +331,60 @@
             x_imag[q % 2, rows, lanes] = mi.astype(BF16)
             x_sum[q % 2, rows, lanes] = (mr + mi).astype(BF16)
 
-    def finish(q, both, first, second):
+    def finish(q, begin, count, both, first, second):
         at = pl.ds(q * width, width)
-        inc_r, inc_i = inc[0, :, at], inc[1, :, at]
+        own = pl.ds(begin, count)
+        inc_r, inc_i = inc[0, own, at], inc[1, own, at]
         total_r = inc_r + (both - second)
         total_i = inc_i + (both + first)
-        mr, mi = spread[0, :, at], spread[1, :, at]
+        mr, mi = spread[0, own, at], spread[1, own, at]
         out_r = mr * total_r - mi * total_i
         out_i = mr * total_i + mi * total_r
         terms = inc_r * out_r + inc_i * out_i
-        terms = jnp.sum(terms.reshape(modes // 8, 8, width), 0)
+        terms = jnp.sum(terms.reshape(count // 8, 8, width), 0)
         part[...] += terms[:, :LANES] + terms[:, LANES:]
-        even = (lax.broadcasted_iota(jnp.int32, (modes, LANES), 1) // dirs) % 2 == 0
+        even = (lax.broadcasted_iota(jnp.int32, (count, LANES), 1) // dirs) % 2 == 0
         for p, out in ((0, out_r), (1, out_i)):
             left, right = out[:, :LANES], out[:, LANES:]
             head = jnp.where(even, left, right)
             tail = pltpu.roll(jnp.where(even, right, left), LANES - dirs, 1)
-            rows = pl.ds(p * modes, modes)
+            rows = pl.ds(p * modes + begin, count)
             scattered[rows, pl.ds(q * width, LANES)] = head.astype(BF16)
             scattered[rows, pl.ds(q * width + LANES, LANES)] = tail.astype(BF16)
 
     part[...] = jnp.zeros_like(part)
-    for work in build(0):
-        work()
     pairs_of = ((t_real, x_sum), (t_diff, x_real), (t_sum, x_imag))
     deep = classes * modes // DEPTH
+    values = {}
+
+    def multiply(q, n, i, rows=slice(0, modes)):
+        matrix, mixed = pairs_of[n]
+        at = slice(i * DEPTH, (i + 1) * DEPTH)
+        term = jnp.dot(matrix[rows, at], mixed[q % 2, at, :], preferred_element_type=F32)
+        values[n] = values[n] + term if i else term
+
+    first = build(0)
+    begun = [0] * 3
+    for n, work in enumerate(first):
+        work()
+        ready = (n + 1) * classes // len(first) * modes if (n + 1) % (len(first) * 2 // classes) == 0 else 0
+        for m in range(1):
+            while (begun[m] + 1) * DEPTH <= ready:
+                multiply(0, m, begun[m])
+                begun[m] += 1
     for q in range(steps):
         todo = build(q + 1) if q + 1 < steps else []
         done = 0
-        results = []
-        for n, (matrix, mixed) in enumerate(pairs_of):
-            value = None
-            for i in range(deep):
-                at = slice(i * DEPTH, (i + 1) * DEPTH)
-                term = jnp.dot(matrix[:, at], mixed[q % 2, at, :], preferred_element_type=F32)
-                value = term if value is None else value + term
-                while done < (n * deep + i + 1) * len(todo) // (3 * deep):
+        count = modes // SPLIT if 0 < q == steps - 1 else modes
+        for begin in range(0, modes, count):
+            rest = [(n, i) for n in range(3) for i in range(begun[n], deep)]
+            for at, (n, i) in enumerate(rest):
+                multiply(q, n, i, slice(begin, begin + count))
+                while done < (at + 1) * len(todo) // len(rest):
                     todo[done]()
                     done += 1
-            results.append(value)
-        finish(q, *results)
+            begun = [0] * 3
+            finish(q, begin, count, *(values[n] for n in range(3)))
 
     row = jnp.sum(part[...], 0, keepdims=True)
     part[0:1, :] = row
@@ -380,7 +397,7 @@
         copy.start()
         sends.append(copy)
     inbox[me] = row
-    for copy in copies:
+    for copy in copies[0] + copies[1]:
         copy.wait_send()
     for copy in sends:
         copy.wait_recv()

time: 39.7 us -> 38.8 us (0.977)
  Pallas kernels: 37.1 us -> 36.2 us
    pallas_call x1, Pallas kernels: 37.1 us -> 36.2 us  [shards(): pl.pallas_call(functools.partial(fused_kernel, dims), out_shape=[jax.Shap...]
where the time goes in v4:
time: 38.8 us; the launch traced here: 38.6 us
  Pallas kernels  36.2 us (93%)
  local copies, waits for them, and re-layouts  1.74 us (4%)
  between operations  0.64 us (2%)
    pallas_call x1, Pallas kernels, shards(): pl.pallas_call(functools.partial(fused_kernel, dims), out_shape=[jax.Shap...  36.2 us
    unnamed x1, local copies, waits for them, and re-layouts  1.23 us

profile of v4, /device:TPU:0, one launch (start us, length us, event | category | flops | bytes accessed | tf_op | source)
XLA Modules:
  0.0 38.6 jit_solution(15237994171452905585)
XLA Ops:
  0.6 36.2 %fused.1 = (bf16[896,1024]{1,0:T(8,128)(2,1)S(1)}, f32[1,128]{1,0:T(1,128)S(1)}) custom-call(s32[1,64]{1,0:T(1,128)} %bitcast.12, s32[1,64]{1,0:T(1,128)} %bitcast.13, s32[1,64]{1,0:T(1,128)} %bitcast.14, s32[1,64]{1,0:T(1,128)} %bitcast.15, f32[3,32]{1,0:T(4,128)} %bitcast.11, f32[3,256]{1,0:T(4,128)} %bitcast.10, s32[32]{0:T(128)} %dir_hbm.1, ...), custom_call_target="tpu_custom_call" | custom-call | tf_op jit(solution)/shard_map/fused/pallas_call | solution.py:440
  36.9 0.5 %slice_bitcast_fusion = f32[32]{0:T(128)} fusion(f32[1,128]{1,0:T(1,128)S(1)} %get-tuple-element.5), kind=kLoop, calls=%fused_computation | loop fusion | bytes 256 | tf_op jit(solution)/shard_map/squeeze | solution.py:495
  37.4 1.2 %copy.13 = bf16[896,1024]{1,0:T(8,128)(2,1)} copy(bf16[896,1024]{1,0:T(8,128)(2,1)S(1)} %get-tuple-element.8) | data formatting | bytes 3670016

commit v5 on v4

--- a/solution.py
+++ b/solution.py
@@ -285,7 +285,7 @@
         pick, all_mie[...].reshape(total, 2 * modes), preferred_element_type=F32
     )
     for j in range(BLOCK):
-        turned = gathered[j * slots : (j + 1) * slots].T.astype(BF16)
+        turned = gathered[j * slots : (j + 1) * slots].astype(BF16).T
         real, imag = turned[:modes], turned[modes:]
         for g in range(PARTS):
             piece = slice(g * chunk, (g + 1) * chunk)

time: 38.8 us -> 38.7 us (level)
  no operation moved by 1% of the time
where the time goes in v5:
time: 38.7 us; the launch traced here: 38.6 us
  Pallas kernels  36.2 us (94%)
  local copies, waits for them, and re-layouts  1.74 us (4%)
  between operations  0.64 us (2%)
    pallas_call x1, Pallas kernels, shards(): pl.pallas_call(functools.partial(fused_kernel, dims), out_shape=[jax.Shap...  36.2 us
    unnamed x1, local copies, waits for them, and re-layouts  1.23 us

profile of v5, /device:TPU:0, one launch (start us, length us, event | category | flops | bytes accessed | tf_op | source)
XLA Modules:
  0.0 38.6 jit_solution(9206685309531707157)
XLA Ops:
  0.6 36.2 %fused.1 = (bf16[896,1024]{1,0:T(8,128)(2,1)S(1)}, f32[1,128]{1,0:T(1,128)S(1)}) custom-call(s32[1,64]{1,0:T(1,128)} %bitcast.12, s32[1,64]{1,0:T(1,128)} %bitcast.13, s32[1,64]{1,0:T(1,128)} %bitcast.14, s32[1,64]{1,0:T(1,128)} %bitcast.15, f32[3,32]{1,0:T(4,128)} %bitcast.11, f32[3,256]{1,0:T(4,128)} %bitcast.10, s32[32]{0:T(128)} %dir_hbm.1, ...), custom_call_target="tpu_custom_call" | custom-call | tf_op jit(solution)/shard_map/fused/pallas_call | solution.py:440
  36.8 0.5 %slice_bitcast_fusion = f32[32]{0:T(128)} fusion(f32[1,128]{1,0:T(1,128)S(1)} %get-tuple-element.5), kind=kLoop, calls=%fused_computation | loop fusion | bytes 256 | tf_op jit(solution)/shard_map/squeeze | solution.py:495
  37.4 1.2 %copy.13 = bf16[896,1024]{1,0:T(8,128)(2,1)} copy(bf16[896,1024]{1,0:T(8,128)(2,1)S(1)} %get-tuple-element.8) | data formatting | bytes 3670016
